TPU v7x, 32 devices: a whole 2x2x4 slice. The times are simulated.
32 devices in a mesh: gx: 4 (over y, x), gy: 2 (over core), ha: 4 (over z).
Axes of the slice: x: 2, y: 2, z: 4, core: 2. Of those that a mesh axis runs over, the one named last changes fastest.
Arguments:
- level_set: float32 [32, 32, 40, 128], P('gx', 'gy', 'ha'), may hold values from -4 to 4
- wind_field: float32 [2, 32, 32], P(None, 'gx', 'gy'), may hold values from -3 to 3
Outputs:
- increment: float32 [32, 32, 40, 128], P('gx', 'gy', 'ha')
All inputs are finite; a program needn't handle non-finite values.
Results may differ from a plain program's by a relative error of at most 0.000073.
Values sent between devices are 32-bit elements; how exact they have to be, the bound alone decides.
A program may use at most 128 MiB of HBM per device.

v0:
```python
import functools
import math

import jax
import jax.numpy as jnp
import numpy as np
from jax import lax
from jax.experimental import pallas as pl
from jax.experimental.pallas import tpu as pltpu
from jax.sharding import PartitionSpec as P

CELL_SIZE = 0.05
SPEED_LOW = 0.1
SPEED_SPAN = 0.4
TURN_MAX = 1.0
ACCEL_MAX = 0.05
CFL_NUMBER = 0.5
WENO_EPS = 1e-06
SCALE = 32.0
PAD = 8
MESH = pl.DeviceIdType.MESH


def rcp(d):
    x = pl.reciprocal(d, approx=True)
    return x * (2.0 - d * x)


def eps_of(spacing):
    return 0.75 * WENO_EPS * (spacing * SCALE) ** 2


def upwind(dm2, dm1, d0, dp1, dp2, c0, c1, fh, eps):
    pos = fh > 0.0
    d1 = jnp.where(pos, dp2, dm2)
    d2 = jnp.where(pos, dp1, dm1)
    d4 = jnp.where(pos, dm1, dp1)
    c = jnp.where(pos, c1, c0)
    d3 = d0
    e1 = d2 - d1
    e2 = d3 - d2
    e3 = d4 - d3
    g2 = 0.75 * d2
    g3 = 0.75 * d3
    s1 = e1 * e1 + (g2 * (d2 + e1) + eps)
    s2 = e2 * e2 + (g2 * d3 + eps)
    s3 = e3 * e3 + (g3 * (d3 - e3) + eps)
    t1 = s2 * s3
    t2 = s1 * s3
    t3 = s1 * s2
    r1 = t1 * t1
    r2 = t2 * t2
    w3 = 1.5 * (t3 * t3)
    num = r1 * (e1 - e2) + w3 * (e2 - e3)
    den = (r1 + 6.0 * r2) + (w3 + w3)
    q = (d3 + 0.5 * d2) + num * rcp(den)
    return q * (jnp.abs(fh) * (1.0 / 3.0)) - c * fh


def triple(da, db, eps):
    e = db - da
    s2 = e * e + (0.75 * (da * db) + eps)
    h = 1.5 * e
    return e, s2 + db * h, s2, s2 - da * h


def face_pair(c, d2, d3, e1, e2, e3, s1, s2, s3):
    t1 = s2 * s3
    t2 = s1 * s3
    t3 = s1 * s2
    r1 = t1 * t1
    r2 = t2 * t2
    r3 = t3 * t3
    a = r1 * (e1 - e2)
    b = r3 * (e2 - e3)
    m = 6.0 * r2 + (r1 + r3)
    n = a + b
    left = (3.0 * c + (d3 + 0.5 * d2)) + (n + 0.5 * b) * rcp(m + (r3 + r3))
    right = ((d2 + 0.5 * d3) - 3.0 * c) + (n + 0.5 * a) * rcp(m + (r1 + r1))
    return left, right


def kernel(sizes, axes, u_ref, wind_ref, flow_ref, rate_ref, out_ref,
           b0, b1, b2, acc, shifted, rights, wind, best, peers, step, sends, recvs, rsend, rrecv):
    nx, ny, nh, nv = sizes
    ngx, ngy, nha = axes
    bufs = (b0, b1, b2)
    d_theta = 2.0 * math.pi / (nh * nha)
    d_speed = SPEED_SPAN / nv
    tiles = ny // 8
    gx, gy, ha = lax.axis_index("gx"), lax.axis_index("gy"), lax.axis_index("ha")
    n_xy = ngx * ngy
    me = gx * ngy + gy

    def peer(delta):
        other = lax.rem(me + delta, n_xy)
        return {"gx": other // ngy, "gy": lax.rem(other, ngy)}

    up_ha = {"ha": lax.rem(ha + 1, nha)}
    down_ha = {"ha": lax.rem(ha + nha - 1, nha)}
    barrier = pltpu.get_barrier_semaphore()
    for delta in range(1, n_xy):
        pl.semaphore_signal(barrier, inc=1, device_id=peer(delta), device_id_type=MESH)
    for target in (up_ha, down_ha):
        pl.semaphore_signal(barrier, inc=1, device_id=target, device_id_type=MESH)

    def load_plane(x, carry):
        for k in range(nh):
            b0[3 + x, 3 + k, PAD:PAD + ny, :] = u_ref[x, k] * SCALE
        for comp in range(2):
            for y in range(ny):
                wind[comp, x, y:y + 1, :] = jnp.full((1, nv), wind_ref[comp, x, y], jnp.float32)
        return carry

    lax.fori_loop(0, nx, load_plane, 0)

    def rate_plane(x, top):
        for r in range(rate_ref.shape[1]):
            for t in range(tiles):
                fx = rate_ref[0, r:r + 1, :] + wind[0, x, 8 * t:8 * t + 8, :]
                fy = rate_ref[1, r:r + 1, :] + wind[1, x, 8 * t:8 * t + 8, :]
                top = jnp.maximum(top, (jnp.abs(fx) + jnp.abs(fy)) * (1.0 / CELL_SIZE))
        return top

    best[...] = lax.fori_loop(0, nx, rate_plane, jnp.zeros((8, 128), jnp.float32))

    pl.semaphore_wait(barrier, n_xy + 1)

    xs, hs, ys = pl.ds(3, nx), pl.ds(3, nh), pl.ds(PAD, ny)

    parts = math.gcd(nh, 5)
    part = nh // parts

    def copies(s):
        buf = bufs[s]
        plans = (
            (buf.at[xs, pl.ds(nh, 3), ys], buf.at[xs, pl.ds(0, 3), ys], up_ha, None, None),
            (buf.at[xs, pl.ds(3, 3), ys], buf.at[xs, pl.ds(3 + nh, 3), ys], down_ha, None, None),
            (buf.at[xs, hs, pl.ds(ny, PAD)], buf.at[xs, hs, pl.ds(0, PAD)], {"gy": gy + 1},
             gy < ngy - 1, gy > 0),
            (buf.at[xs, hs, pl.ds(PAD, PAD)], buf.at[xs, hs, pl.ds(PAD + ny, PAD)], {"gy": gy - 1},
             gy > 0, gy < ngy - 1),
        )
        for c in range(parts):
            hc = pl.ds(3 + c * part, part)
            plans += (
                (buf.at[pl.ds(nx, 3), hc, ys], buf.at[pl.ds(0, 3), hc, ys], {"gx": gx + 1},
                 gx < ngx - 1, gx > 0),
                (buf.at[pl.ds(3, 3), hc, ys], buf.at[pl.ds(3 + nx, 3), hc, ys], {"gx": gx - 1},
                 gx > 0, gx < ngx - 1),
            )
        return [
            (pltpu.make_async_remote_copy(
                src_ref=src, dst_ref=dst, send_sem=sends.at[s, i], recv_sem=recvs.at[s, i],
                device_id=target, device_id_type=MESH), has_out, has_in)
            for i, (src, dst, target, has_out, has_in) in enumerate(plans)
        ]

    def under(condition, act):
        if condition is None:
            act()
        else:
            pl.when(condition)(act)

    rate_copies = [
        pltpu.make_async_remote_copy(
            src_ref=best, dst_ref=peers.at[delta - 1], send_sem=rsend.at[delta - 1],
            recv_sem=rrecv.at[delta - 1], device_id=peer(delta), device_id_type=MESH)
        for delta in range(1, n_xy)
    ]
    plans = [copies(s) for s in range(3)]

    def send(s, which):
        for i in which:
            copy, has_out, _ = plans[s][i]
            under(has_out, copy.start)

    def wait_in(s, which):
        for i in which:
            copy, _, has_in = plans[s][i]
            under(has_in, copy.wait_recv)

    def v_shift(buf):
        def body(i, carry):
            for j in range(2):
                for k in range(nh):
                    u = buf[3 + 2 * i + j, 3 + k, PAD:PAD + ny, :]
                    for at, move in enumerate((3, 2, 1, nv - 1, nv - 2)):
                        shifted[at, 2 * i + j, k] = pltpu.roll(u, move, 1)
            return carry

        lax.fori_loop(0, nx // 2, body, 0)

    def v_pass(buf):
        eps = eps_of(d_speed)
        coef = ACCEL_MAX / (3.0 * d_speed)
        e4 = np.float32(np.float32(eps * eps) ** 2)
        lane = lax.broadcasted_iota(jnp.int32, (8, nv), 1)
        edge = lane == 0
        keep1 = jnp.where((lane == 1) | (lane == 2), 0.0, 1.0)
        keep2 = jnp.where(lane < 2, 0.0, 1.0)
        keep3 = jnp.where((lane == 0) | (lane == nv - 1), 0.0, 1.0)
        keep4 = jnp.where(lane >= nv - 2, 0.0, 1.0)
        inner_lane = jnp.where(edge, 0.0, 1.0)

        def one(x, k, t):
            rows = slice(8 * t, 8 * t + 8)
            u0 = buf[3 + x, 3 + k, PAD + 8 * t:PAD + 8 * t + 8, :]
            um3, um2, um1, up1, up2 = [shifted[at, x, k, rows, :] for at in range(5)]
            qa, qb, qc, qd, qe = um2 - um3, um1 - um2, u0 - um1, up1 - u0, up2 - up1
            d1 = (qb - qa) * keep1
            d2 = (qc - qb) * keep2
            d3 = (qd - qc) * keep3
            d4 = (qe - qd) * keep4
            e1 = d2 - d1
            e2 = d3 - d2
            e3 = d4 - d3
            g2 = 0.75 * d2
            g3 = 0.75 * d3
            s1 = e1 * e1 + (g2 * (d2 + e1) + eps)
            s2 = e2 * e2 + (g2 * d3 + eps)
            s3 = e3 * e3 + (g3 * (d3 - e3) + eps)
            t1 = s2 * s3
            t2 = s1 * s3
            t3 = s1 * s2
            r1 = t1 * t1
            r2 = t2 * t2
            r3 = t3 * t3
            f12 = e1 - e2
            f23 = e2 - e3
            r2l = jnp.where(edge, r1, r2)
            r3l = jnp.where(edge, e4, r3)
            r2r = jnp.where(edge, r3, r2)
            r1r = jnp.where(edge, e4, r1)
            cl = jnp.where(edge, qd, qc)
            cr = jnp.where(edge, qb, qc)
            nl = r1 * (f12 * inner_lane) + 1.5 * (r3l * f23)
            nr = 1.5 * (r1r * f12) + r3 * (f23 * inner_lane)
            left = (3.0 * cl + (d3 + 0.5 * d2)) + nl * rcp(r1 + 6.0 * r2l + 3.0 * r3l)
            right = ((d2 + 0.5 * d3) - 3.0 * cr) + nr * rcp(3.0 * r1r + 6.0 * r2r + r3)
            acc[x, k, rows, :] = coef * left
            rights[x, k, rows, :] = coef * right

        def body(x, carry):
            def inner(k, carry):
                for j in range(2):
                    for t in range(tiles):
                        one(x, 2 * k + j, t)
                return carry
            return lax.fori_loop(0, nh // 2, inner, carry)

        lax.fori_loop(0, nx, body, 0)

    def h_pass(buf):
        eps = eps_of(d_theta)
        coef = TURN_MAX / (3.0 * d_theta)

        def body(i, carry):
            x = i // tiles
            rows = pl.ds(pl.multiple_of(lax.rem(i, tiles) * 8, 8) + PAD, 8)
            rows_acc = pl.ds(pl.multiple_of(lax.rem(i, tiles) * 8, 8), 8)
            u = [buf[3 + x, j, rows, :] for j in range(nh + 6)]
            q = [u[j + 1] - u[j] for j in range(nh + 5)]
            d = [q[j + 1] - q[j] for j in range(nh + 4)]
            tr = [triple(d[j], d[j + 1], eps) for j in range(nh + 3)]
            before = None
            for f in range(nh + 1):
                left, right = face_pair(
                    q[f + 2], d[f + 1], d[f + 2], tr[f][0], tr[f + 1][0], tr[f + 2][0],
                    tr[f][1], tr[f + 1][2], tr[f + 2][3])
                if before is not None:
                    acc[x, f - 1, rows_acc, :] += coef * jnp.minimum(before, right)
                before = left
            return carry

        lax.fori_loop(0, nx * tiles, body, 0)

    def flow_row(comp, k):
        return flow_ref[comp, pl.ds(ha * nh + k, 1), :]

    def y_pass(buf):
        eps = eps_of(CELL_SIZE)

        group = math.gcd(nh, 5)

        def one(x, k, row, t):
            u = [buf[3 + x, 3 + k, PAD + 8 * t + j:PAD + 8 * t + j + 8, :] for j in range(-3, 4)]
            q = [u[j + 1] - u[j] for j in range(6)]
            d = [q[j + 1] - q[j] for j in range(5)]
            fh = (row + wind[1, x, 8 * t:8 * t + 8, :]) * (1.0 / CELL_SIZE)
            return upwind(*d, q[2], q[3], fh, eps)

        def body(x, carry):
            def inner(g, carry):
                speed = [pltpu.roll(rights[x, group * g + j], nv - 1, 1) for j in range(group)]
                for j in range(group):
                    k = group * g + j
                    row = flow_row(1, k)
                    for t in range(tiles):
                        rows = slice(8 * t, 8 * t + 8)
                        along_v = jnp.minimum(acc[x, k, rows, :], speed[j][rows])
                        acc[x, k, rows, :] = along_v + one(x, k, row, t)
                return carry
            return lax.fori_loop(0, nh // group, inner, carry)

        lax.fori_loop(0, nx, body, 0)

    def x_pass(s):
        buf = bufs[s]
        eps = eps_of(CELL_SIZE)

        def body(first, i, carry):
            k = first + i // tiles
            base = pl.multiple_of(lax.rem(i, tiles) * 8, 8)
            rows, rows_acc = pl.ds(base + PAD, 8), pl.ds(base, 8)
            row = flow_row(0, k)
            dt = step[...]
            u = [buf[j, 3 + k, rows, :] for j in range(nx + 6)]
            q = [u[j + 1] - u[j] for j in range(nx + 5)]
            d = [q[j + 1] - q[j] for j in range(nx + 4)]
            for x in range(nx):
                fh = (row + wind[0, x, rows_acc, :]) * (1.0 / CELL_SIZE)
                total = acc[x, k, rows_acc, :] + upwind(*d[x:x + 5], q[x + 2], q[x + 3], fh, eps)
                moved = u[x + 3] - dt * jnp.maximum(total, 0.0)
                if s == 0:
                    b1[3 + x, 3 + k, rows, :] = moved
                elif s == 1:
                    b2[3 + x, 3 + k, rows, :] = 0.75 * b0[3 + x, 3 + k, rows, :] + 0.25 * moved
                else:
                    out_ref[x, k, rows_acc, :] = (moved - b0[3 + x, 3 + k, rows, :]) * (2.0 / (3.0 * SCALE))
            return carry

        for c in range(parts):
            mine = (4 + 2 * c, 5 + 2 * c)
            wait_in(s, mine)
            lax.fori_loop(0, part * tiles, functools.partial(body, c * part), 0)
            if s < 2:
                send(s + 1, mine)
        if s < 2:
            send(s + 1, range(4))

    def fill_x(buf):
        def ends(low):
            def act():
                def body(k, carry):
                    edge = buf[3 if low else nx + 2, 3 + k, PAD:PAD + ny, :]
                    slope = edge - buf[4 if low else nx + 1, 3 + k, PAD:PAD + ny, :]
                    for r in range(1, 4):
                        buf[3 - r if low else nx + 2 + r, 3 + k, PAD:PAD + ny, :] = edge + r * slope
                    return carry
                lax.fori_loop(0, nh, body, 0)
            return act
        pl.when(gx == 0)(ends(True))
        pl.when(gx == ngx - 1)(ends(False))

    def fill_y(buf):
        index = lax.broadcasted_iota(jnp.int32, (8, nv), 0).astype(jnp.float32)

        def ends(low):
            reach = (8.0 - index) if low else (index + 1.0)
            at, near, to = (PAD, PAD + 1, 0) if low else (PAD + ny - 1, PAD + ny - 2, PAD + ny)

            def act():
                def body(x, carry):
                    for k in range(nh):
                        edge = buf[3 + x, 3 + k, at:at + 1, :]
                        slope = edge - buf[3 + x, 3 + k, near:near + 1, :]
                        buf[3 + x, 3 + k, to:to + 8, :] = edge + reach * slope
                    return carry
                lax.fori_loop(0, nx, body, 0)
            return act
        pl.when(gy == 0)(ends(True))
        pl.when(gy == ngy - 1)(ends(False))

    for s in range(3):
        if s == 0:
            send(0, range(4 + 2 * parts))
            for copy in rate_copies:
                copy.start()
        v_shift(bufs[s])
        v_pass(bufs[s])
        fill_y(bufs[s])
        fill_x(bufs[s])
        wait_in(s, (2, 3))
        y_pass(bufs[s])
        wait_in(s, (0, 1))
        h_pass(bufs[s])
        if s == 0:
            for copy in rate_copies:
                copy.wait_recv()
            top = best[...]
            for delta in range(1, n_xy):
                top = jnp.maximum(top, peers[delta - 1])
            rate = jnp.max(top, axis=(0, 1), keepdims=True) + (TURN_MAX / d_theta + ACCEL_MAX / d_speed)
            step[...] = jnp.broadcast_to(CFL_NUMBER / rate, step.shape)
        x_pass(s)

    for copy in rate_copies:
        copy.wait_send()
    for s in range(3):
        for copy, has_out, _ in plans[s]:
            under(has_out, copy.wait_send)


def tables(nv, n_head):
    speeds = (SPEED_LOW + SPEED_SPAN * (np.arange(nv, dtype=np.float32) + np.float32(0.5)) / nv).astype(np.float32)
    angles = np.arange(n_head, dtype=np.float32) * np.float32(2.0 * math.pi / n_head)
    turns = np.stack([np.cos(angles.astype(np.float64)), np.sin(angles.astype(np.float64))]).astype(np.float32)
    flow = turns[:, :, None] * speeds[None, None, :]
    ends = np.concatenate([flow[:, :, 0], flow[:, :, -1]], axis=1)
    rows = -(-ends.shape[1] // 128)
    ends = np.concatenate([ends, np.repeat(ends[:, :1], rows * 128 - ends.shape[1], axis=1)], axis=1)
    return flow, ends.reshape(2, rows, 128)


def solution(mesh):
    axes = (mesh.shape["gx"], mesh.shape["gy"], mesh.shape["ha"])

    def body(level_set, wind_field):
        nx, ny, nh, nv = level_set.shape
        flow, ends = tables(nv, nh * axes[2])
        n_xy = axes[0] * axes[1]
        state = pltpu.VMEM((nx + 6, nh + 6, ny + 2 * PAD, nv), jnp.float32)
        vmem = pl.BlockSpec(memory_space=pltpu.VMEM)
        increment = pl.pallas_call(
            functools.partial(kernel, (nx, ny, nh, nv), axes),
            out_shape=jax.ShapeDtypeStruct((nx, nh, ny, nv), jnp.float32),
            in_specs=[vmem, pl.BlockSpec(memory_space=pltpu.SMEM), vmem, vmem],
            out_specs=vmem,
            scratch_shapes=[
                state, state, state,
                pltpu.VMEM((nx, nh, ny, nv), jnp.float32),
                pltpu.VMEM((5, nx, nh, ny, nv), jnp.float32),
                pltpu.VMEM((nx, nh, ny, nv), jnp.float32),
                pltpu.VMEM((2, nx, ny, nv), jnp.float32),
                pltpu.VMEM((8, 128), jnp.float32),
                pltpu.VMEM((n_xy - 1, 8, 128), jnp.float32),
                pltpu.VMEM((8, nv), jnp.float32),
                pltpu.SemaphoreType.DMA((3, 4 + 2 * math.gcd(nh, 5))),
                pltpu.SemaphoreType.DMA((3, 4 + 2 * math.gcd(nh, 5))),
                pltpu.SemaphoreType.DMA((n_xy - 1,)),
                pltpu.SemaphoreType.DMA((n_xy - 1,)),
            ],
            compiler_params=pltpu.CompilerParams(
                collective_id=0, has_side_effects=True, vmem_limit_bytes=56 * 2**20
            ),
        )(level_set.transpose(0, 2, 1, 3), wind_field, jnp.asarray(flow), jnp.asarray(ends))
        return increment.transpose(0, 2, 1, 3)

    return jax.shard_map(
        body,
        mesh=mesh,
        in_specs=(P("gx", "gy", "ha", None), P(None, "gx", "gy")),
        out_specs=P("gx", "gy", "ha", None),
        check_vma=False,
    )
```

profile of v0, /device:TPU:0, one launch (start us, length us, event | category | flops | bytes accessed | tf_op | source)
XLA Modules:
  0.0 51.4 jit_solution(9297858308816940)
XLA Ops:
  0.0 49.4 %shard_map.46 = f32[8,10,16,128]{3,2,1,0:T(8,128)} custom-call(f32[8,10,16,128]{3,2,1,0:T(8,128)} %bitcast.3, f32[2,8,16]{2,1,0:T(8,128)} %wind_ref.1, f32[2,40,128]{2,1,0:T(8,128)} %constant.4.clone.flow_ref, f32[2,1,128]{2,1,0:T(1,128)} %constant.5.clone.rate_ref), custom_call_target="tpu_custom_call" | custom-call | tf_op jit(solution)/shard_map/pallas_call | solution.py:425
  49.4 2.0 %copy.6 = f32[8,16,10,128]{3,1,2,0:T(8,128)} copy(f32[8,16,10,128]{3,1,2,0:T(8,128)} %bitcast.2) | data formatting | bytes 1310720
where the time goes:
time: 51.5 us; the launch traced here: 51.4 us
  Pallas kernels  49.4 us (96%)
  local copies, waits for them, and re-layouts  1.97 us (4%)
    pallas_call x1, Pallas kernels, body(): pl.pallas_call(functools.partial(kernel, (nx, ny, nh, nv), axes), out_sha...  49.4 us
    unnamed x1, local copies, waits for them, and re-layouts  1.97 us

commit v1 on v0

v1 whole, which is shorter than its diff:
```python
import functools
import math

import jax
import jax.numpy as jnp
import numpy as np
from jax import lax
from jax.experimental import pallas as pl
from jax.experimental.pallas import tpu as pltpu
from jax.sharding import PartitionSpec as P

CELL_SIZE = 0.05
SPEED_LOW = 0.1
SPEED_SPAN = 0.4
TURN_MAX = 1.0
ACCEL_MAX = 0.05
CFL_NUMBER = 0.5
WENO_EPS = 1e-06
SCALE = 32.0
PAD = 8
MESH = pl.DeviceIdType.MESH


def rcp(d):
    return pl.reciprocal(d, approx=False)


def eps_of(spacing):
    return 0.75 * WENO_EPS * (spacing * SCALE) ** 2


def smooth(d2, d3, e1, e2, e3, eps):
    g2 = 0.75 * d2
    g3 = 0.75 * d3
    c3 = g3 * d3 + eps
    s1 = e1 * (e1 + g2) + (g2 * d2 + eps)
    s2 = e2 * (e2 - g3) + c3
    s3 = e3 * (e3 - g3) + c3
    return s1, s2, s3


def upwind(dm2, dm1, d0, dp1, dp2, c0, c1, fh, eps):
    pos = fh > 0.0
    d1 = jnp.where(pos, dp2, dm2)
    d2 = jnp.where(pos, dp1, dm1)
    d4 = jnp.where(pos, dm1, dp1)
    c = jnp.where(pos, c1, c0)
    d3 = d0
    e1 = d2 - d1
    e2 = d3 - d2
    e3 = d4 - d3
    s1, s2, s3 = smooth(d2, d3, e1, e2, e3, eps)
    t1 = s2 * s3
    t2 = s1 * s3
    t3 = s1 * s2
    r1 = t1 * t1
    r2 = t2 * t2
    w3 = 1.5 * (t3 * t3)
    num = r1 * (e1 - e2) + w3 * (e2 - e3)
    den = (r1 + 6.0 * r2) + (w3 + w3)
    q = (d3 + 0.5 * d2) + num * rcp(den)
    return q * (jnp.abs(fh) * (1.0 / 3.0)) - c * fh


def triple(da, db, eps):
    e = db - da
    s2 = e * e + (0.75 * (da * db) + eps)
    h = 1.5 * e
    return e, s2 + db * h, s2, s2 - da * h


def face_pair(c, d2, d3, e1, e2, e3, s1, s2, s3):
    t1 = s2 * s3
    t2 = s1 * s3
    t3 = s1 * s2
    r1 = t1 * t1
    r2 = t2 * t2
    r3 = t3 * t3
    a = r1 * (e1 - e2)
    b = r3 * (e2 - e3)
    m = 6.0 * r2 + (r1 + r3)
    n = a + b
    left = (3.0 * c + (d3 + 0.5 * d2)) + (n + 0.5 * b) * rcp(m + (r3 + r3))
    right = ((d2 + 0.5 * d3) - 3.0 * c) + (n + 0.5 * a) * rcp(m + (r1 + r1))
    return left, right


def head_chunks(nh):
    return ((0, 3), (nh - 3, 3), (3, nh - 6))


def plane_chunks(nx):
    half = nx // 2
    return ((0, half), (half, nx - half))


def n_copies(nx, nh, tiles):
    return 2 * tiles * len(plane_chunks(nx)) + 2 * len(head_chunks(nh)) * (tiles + 1)


def kernel(sizes, axes, u_ref, wind_ref, flow_ref, rate_ref, out_hbm,
           b0, b1, b2, acc, rights, out_ref, va, vb, wind, best, peers, step,
           sends, recvs, rsend, rrecv, osem):
    nx, ny, nh, nv = sizes
    ngx, ngy, nha = axes
    bufs = (b0, b1, b2)
    d_theta = 2.0 * math.pi / (nh * nha)
    d_speed = SPEED_SPAN / nv
    tiles = ny // 8
    group = nh // 2
    heads, planes = head_chunks(nh), plane_chunks(nx)
    gx, gy, ha = lax.axis_index("gx"), lax.axis_index("gy"), lax.axis_index("ha")
    n_xy = ngx * ngy
    me = gx * ngy + gy

    def peer(delta):
        other = lax.rem(me + delta, n_xy)
        return {"gx": other // ngy, "gy": lax.rem(other, ngy)}

    up_ha = {"ha": lax.rem(ha + 1, nha)}
    down_ha = {"ha": lax.rem(ha + nha - 1, nha)}
    barrier = pltpu.get_barrier_semaphore()
    for delta in range(1, n_xy):
        pl.semaphore_signal(barrier, inc=1, device_id=peer(delta), device_id_type=MESH)
    for target in (up_ha, down_ha):
        pl.semaphore_signal(barrier, inc=1, device_id=target, device_id_type=MESH)

    def load_plane(x, carry):
        for k in range(nh):
            b0[3 + x, 3 + k, PAD:PAD + ny, :] = u_ref[x, k] * SCALE
        for comp in range(2):
            for y in range(ny):
                wind[comp, x, y:y + 1, :] = jnp.full((1, nv), wind_ref[comp, x, y] * (1.0 / CELL_SIZE), jnp.float32)
        return carry

    lax.fori_loop(0, nx, load_plane, 0)

    def rate_plane(x, top):
        for r in range(rate_ref.shape[1]):
            for t in range(tiles):
                fx = rate_ref[0, r:r + 1, :] + wind[0, x, 8 * t:8 * t + 8, :]
                fy = rate_ref[1, r:r + 1, :] + wind[1, x, 8 * t:8 * t + 8, :]
                top = jnp.maximum(top, jnp.abs(fx) + jnp.abs(fy))
        return top

    best[...] = lax.fori_loop(0, nx, rate_plane, jnp.zeros((8, 128), jnp.float32))

    pl.semaphore_wait(barrier, n_xy + 1)

    def tile_rows(t):
        return pl.ds(PAD + 8 * t, 8)

    def copies(s):
        buf = bufs[s]
        plans = {}
        for t in range(tiles):
            ys = tile_rows(t)
            for c, (x0, count) in enumerate(planes):
                xs = pl.ds(3 + x0, count)
                plans["h", t, c] = (
                    (buf.at[xs, pl.ds(nh, 3), ys], buf.at[xs, pl.ds(0, 3), ys], up_ha, None, None),
                    (buf.at[xs, pl.ds(3, 3), ys], buf.at[xs, pl.ds(3 + nh, 3), ys], down_ha, None, None),
                )
            for c, (k0, count) in enumerate(heads):
                hc = pl.ds(3 + k0, count)
                plans["x", t, c] = (
                    (buf.at[pl.ds(nx, 3), hc, ys], buf.at[pl.ds(0, 3), hc, ys], {"gx": gx + 1},
                     gx < ngx - 1, gx > 0),
                    (buf.at[pl.ds(3, 3), hc, ys], buf.at[pl.ds(3 + nx, 3), hc, ys], {"gx": gx - 1},
                     gx > 0, gx < ngx - 1),
                )
        xs = pl.ds(3, nx)
        for c, (k0, count) in enumerate(heads):
            hc = pl.ds(3 + k0, count)
            plans["y", tiles - 1, c] = (
                (buf.at[xs, hc, pl.ds(ny, PAD)], buf.at[xs, hc, pl.ds(0, PAD)], {"gy": gy + 1},
                 gy < ngy - 1, gy > 0),
            )
            plans["y", 0, c] = plans.get(("y", 0, c), ()) + (
                (buf.at[xs, hc, pl.ds(PAD, PAD)], buf.at[xs, hc, pl.ds(PAD + ny, PAD)], {"gy": gy - 1},
                 gy > 0, gy < ngy - 1),
            )
        made, at = {}, 0
        for key, group_of in plans.items():
            row = []
            for src, dst, target, has_out, has_in in group_of:
                row.append((pltpu.make_async_remote_copy(
                    src_ref=src, dst_ref=dst, send_sem=sends.at[s, at], recv_sem=recvs.at[s, at],
                    device_id=target, device_id_type=MESH), has_out, has_in))
                at += 1
            made[key] = row
        return made

    def under(condition, act):
        if condition is None:
            act()
        else:
            pl.when(condition)(act)

    rate_copies = [
        pltpu.make_async_remote_copy(
            src_ref=best, dst_ref=peers.at[delta - 1], send_sem=rsend.at[delta - 1],
            recv_sem=rrecv.at[delta - 1], device_id=peer(delta), device_id_type=MESH)
        for delta in range(1, n_xy)
    ]
    plans = [copies(s) for s in range(3)]

    def send(s, *key):
        for copy, has_out, _ in plans[s].get(key, ()):
            under(has_out, copy.start)

    def wait_in(s, *key):
        for copy, _, has_in in plans[s].get(key, ()):
            under(has_in, copy.wait_recv)

    def v_pass(buf, t):
        eps = eps_of(d_speed)
        coef = ACCEL_MAX / (3.0 * d_speed)
        e4 = np.float32(np.float32(eps * eps) ** 2)
        lane = lax.broadcasted_iota(jnp.int32, (8, nv), 1)
        edge = lane == 0
        keep = jnp.where((lane == 0) | (lane == nv - 1), 0.0, 1.0)
        inner_lane = jnp.where(edge, 0.0, 1.0)
        rows, rows_acc = tile_rows(t), slice(8 * t, 8 * t + 8)

        def first(x, half):
            for j in range(group):
                u = buf[3 + x, 3 + half * group + j, rows, :]
                q = u - pltpu.roll(u, 1, 1)
                va[half, 0, j] = q
                va[half, 1, j] = ((pltpu.roll(u, nv - 1, 1) - u) - q) * keep

        def second(half):
            for j in range(group):
                q, d = va[half, 0, j], va[half, 1, j]
                vb[half, 0, j] = pltpu.roll(d, 2, 1)
                vb[half, 1, j] = pltpu.roll(d, 1, 1)
                vb[half, 2, j] = d
                vb[half, 3, j] = pltpu.roll(d, nv - 1, 1)
                vb[half, 4, j] = pltpu.roll(q, 1, 1)
                vb[half, 5, j] = q
                vb[half, 6, j] = pltpu.roll(q, nv - 1, 1)

        def third(x, half):
            for j in range(group):
                k = half * group + j
                d1, d2, d3, d4, qb, qc, qd = [vb[half, i, j] for i in range(7)]
                e1 = d2 - d1
                e2 = d3 - d2
                e3 = d4 - d3
                s1, s2, s3 = smooth(d2, d3, e1, e2, e3, eps)
                t1 = s2 * s3
                t2 = s1 * s3
                t3 = s1 * s2
                r1 = t1 * t1
                r2 = t2 * t2
                r3 = t3 * t3
                f12 = e1 - e2
                f23 = e2 - e3
                r2l = jnp.where(edge, r1, r2)
                r3l = jnp.where(edge, e4, r3)
                r2r = jnp.where(edge, r3, r2)
                r1r = jnp.where(edge, e4, r1)
                cl = jnp.where(edge, qd, qc)
                cr = jnp.where(edge, qb, qc)
                nl = r1 * (f12 * inner_lane) + 1.5 * (r3l * f23)
                nr = 1.5 * (r1r * f12) + r3 * (f23 * inner_lane)
                left = (3.0 * cl + (d3 + 0.5 * d2)) + nl * rcp(r1 + 6.0 * r2l + 3.0 * r3l)
                right = ((d2 + 0.5 * d3) - 3.0 * cr) + nr * rcp(3.0 * r1r + 6.0 * r2r + r3)
                acc[x, k, rows_acc, :] = coef * left
                rights[x, k, rows_acc, :] = coef * right

        first(0, 0)
        first(0, 1)
        second(0)

        def body(x, carry):
            after = jnp.minimum(x + 1, nx - 1)
            third(x, 0)
            second(1)
            first(after, 0)
            third(x, 1)
            second(0)
            first(after, 1)
            return carry

        lax.fori_loop(0, nx, body, 0)

    def h_pass(s, t):
        buf = bufs[s]
        eps = eps_of(d_theta)
        coef = TURN_MAX / (3.0 * d_theta)
        rows, rows_acc = tile_rows(t), pl.ds(8 * t, 8)

        def body(x, carry):
            u = [buf[3 + x, j, rows, :] for j in range(nh + 6)]
            q = [u[j + 1] - u[j] for j in range(nh + 5)]
            d = [q[j + 1] - q[j] for j in range(nh + 4)]
            tr = [triple(d[j], d[j + 1], eps) for j in range(nh + 3)]
            before = None
            for f in range(nh + 1):
                left, right = face_pair(
                    q[f + 2], d[f + 1], d[f + 2], tr[f][0], tr[f + 1][0], tr[f + 2][0],
                    tr[f][1], tr[f + 1][2], tr[f + 2][3])
                if before is not None:
                    acc[x, f - 1, rows_acc, :] += coef * jnp.minimum(before, right)
                before = left
            return carry

        for c, (x0, count) in enumerate(planes):
            wait_in(s, "h", t, c)
            lax.fori_loop(x0, x0 + count, body, 0)

    def flow_row(comp, k):
        return flow_ref[comp, pl.ds(ha * nh + k, 1), :]

    def y_pass(s, t):
        buf = bufs[s]
        eps = eps_of(CELL_SIZE)
        rows = slice(8 * t, 8 * t + 8)

        def body(x, carry):
            for k in range(nh):
                u = [buf[3 + x, 3 + k, PAD + 8 * t + j:PAD + 8 * t + j + 8, :] for j in range(-3, 4)]
                q = [u[j + 1] - u[j] for j in range(6)]
                d = [q[j + 1] - q[j] for j in range(5)]
                fh = flow_row(1, k) + wind[1, x, rows, :]
                along_v = jnp.minimum(acc[x, k, rows, :], pltpu.roll(rights[x, k, rows, :], nv - 1, 1))
                acc[x, k, rows, :] = along_v + upwind(*d, q[2], q[3], fh, eps)
            return carry

        for c in range(len(heads)):
            if t == 0:
                for copy, _, has_in in plans[s]["y", tiles - 1, c][:1]:
                    under(has_in, copy.wait_recv)
            if t == tiles - 1:
                for copy, _, has_in in plans[s]["y", 0, c][-1:]:
                    under(has_in, copy.wait_recv)
        lax.fori_loop(0, nx, body, 0)

    def out_copy(t, c):
        k0, count = heads[c]
        part = (pl.ds(0, nx), pl.ds(k0, count), pl.ds(8 * t, 8))
        return pltpu.make_async_copy(out_ref.at[part], out_hbm.at[part], osem.at[t, c])

    def x_pass(s, t):
        buf = bufs[s]
        eps = eps_of(CELL_SIZE)
        rows, rows_acc = tile_rows(t), pl.ds(8 * t, 8)

        def body(k, carry):
            row = flow_row(0, k)
            dt = step[...]
            u = [buf[j, 3 + k, rows, :] for j in range(nx + 6)]
            q = [u[j + 1] - u[j] for j in range(nx + 5)]
            d = [q[j + 1] - q[j] for j in range(nx + 4)]
            for x in range(nx):
                fh = row + wind[0, x, rows_acc, :]
                total = acc[x, k, rows_acc, :] + upwind(*d[x:x + 5], q[x + 2], q[x + 3], fh, eps)
                moved = u[x + 3] - dt * jnp.maximum(total, 0.0)
                if s == 0:
                    b1[3 + x, 3 + k, rows, :] = moved
                elif s == 1:
                    b2[3 + x, 3 + k, rows, :] = 0.75 * b0[3 + x, 3 + k, rows, :] + 0.25 * moved
                else:
                    out_ref[x, k, rows_acc, :] = (moved - b0[3 + x, 3 + k, rows, :]) * (2.0 / (3.0 * SCALE))
            return carry

        for c, (k0, count) in enumerate(heads):
            wait_in(s, "x", t, c)
            lax.fori_loop(k0, k0 + count, body, 0)
            if s < 2:
                send(s + 1, "x", t, c)
                send(s + 1, "y", t, c)
                if c == 1:
                    for p in range(len(planes)):
                        send(s + 1, "h", t, p)
            else:
                out_copy(t, c).start()

    def fill_x(buf, t):
        rows = tile_rows(t)

        def ends(low):
            def act():
                def body(k, carry):
                    edge = buf[3 if low else nx + 2, 3 + k, rows, :]
                    slope = edge - buf[4 if low else nx + 1, 3 + k, rows, :]
                    for r in range(1, 4):
                        buf[3 - r if low else nx + 2 + r, 3 + k, rows, :] = edge + r * slope
                    return carry
                lax.fori_loop(0, nh, body, 0)
            return act
        pl.when(gx == 0)(ends(True))
        pl.when(gx == ngx - 1)(ends(False))

    def fill_y(buf, t):
        index = lax.broadcasted_iota(jnp.int32, (8, nv), 0).astype(jnp.float32)

        def ends(low):
            reach = (8.0 - index) if low else (index + 1.0)
            at, near, to = (PAD, PAD + 1, 0) if low else (PAD + ny - 1, PAD + ny - 2, PAD + ny)

            def act():
                def body(x, carry):
                    for k in range(nh):
                        edge = buf[3 + x, 3 + k, at:at + 1, :]
                        slope = edge - buf[3 + x, 3 + k, near:near + 1, :]
                        buf[3 + x, 3 + k, to:to + 8, :] = edge + reach * slope
                    return carry
                lax.fori_loop(0, nx, body, 0)
            return act
        if t == 0:
            pl.when(gy == 0)(ends(True))
        if t == tiles - 1:
            pl.when(gy == ngy - 1)(ends(False))

    for t in range(tiles):
        for p in range(len(planes)):
            send(0, "h", t, p)
        for c in range(len(heads)):
            send(0, "x", t, c)
            send(0, "y", t, c)
        if t == 0:
            for copy in rate_copies:
                copy.start()
    v_pass(b0, 0)
    for s in range(3):
        fill_y(bufs[s], 0)
        fill_y(bufs[s], tiles - 1) if tiles > 1 else None
        y_pass(s, 0)
        for t in range(1, tiles):
            v_pass(bufs[s], t)
            y_pass(s, t)
        for t in range(tiles):
            fill_x(bufs[s], t)
            h_pass(s, t)
            if s == 0 and t == 0:
                for copy in rate_copies:
                    copy.wait_recv()
                top = best[...]
                for delta in range(1, n_xy):
                    top = jnp.maximum(top, peers[delta - 1])
                rate = jnp.max(top, axis=(0, 1), keepdims=True) + (TURN_MAX / d_theta + ACCEL_MAX / d_speed)
                step[...] = jnp.broadcast_to(CFL_NUMBER / rate, step.shape)
            x_pass(s, t)
            if s < 2 and t == 0:
                v_pass(bufs[s + 1], 0)

    for t in range(tiles):
        for c in range(len(heads)):
            out_copy(t, c).wait()
    for copy in rate_copies:
        copy.wait_send()
    for s in range(3):
        for row in plans[s].values():
            for copy, has_out, _ in row:
                under(has_out, copy.wait_send)


def tables(nv, n_head):
    speeds = (SPEED_LOW + SPEED_SPAN * (np.arange(nv, dtype=np.float32) + np.float32(0.5)) / nv).astype(np.float32)
    angles = np.arange(n_head, dtype=np.float32) * np.float32(2.0 * math.pi / n_head)
    turns = np.stack([np.cos(angles.astype(np.float64)), np.sin(angles.astype(np.float64))])
    flow = (turns[:, :, None] * speeds[None, None, :] / CELL_SIZE).astype(np.float32)
    ends = np.concatenate([flow[:, :, 0], flow[:, :, -1]], axis=1)
    rows = -(-ends.shape[1] // 128)
    ends = np.concatenate([ends, np.repeat(ends[:, :1], rows * 128 - ends.shape[1], axis=1)], axis=1)
    return flow, ends.reshape(2, rows, 128)


def solution(mesh):
    axes = (mesh.shape["gx"], mesh.shape["gy"], mesh.shape["ha"])

    def body(level_set, wind_field):
        nx, ny, nh, nv = level_set.shape
        flow, ends = tables(nv, nh * axes[2])
        n_xy = axes[0] * axes[1]
        tiles = ny // 8
        count = n_copies(nx, nh, tiles)
        state = pltpu.VMEM((nx + 6, nh + 6, ny + 2 * PAD, nv), jnp.float32)
        cells = pltpu.VMEM((nx, nh, ny, nv), jnp.float32)
        vmem = pl.BlockSpec(memory_space=pltpu.VMEM)
        increment = pl.pallas_call(
            functools.partial(kernel, (nx, ny, nh, nv), axes),
            out_shape=jax.ShapeDtypeStruct((nx, nh, ny, nv), jnp.float32),
            in_specs=[vmem, pl.BlockSpec(memory_space=pltpu.SMEM), vmem, vmem],
            out_specs=pl.BlockSpec(memory_space=pltpu.HBM),
            scratch_shapes=[
                state, state, state, cells, cells, cells,
                pltpu.VMEM((2, 2, nh // 2, 8, nv), jnp.float32),
                pltpu.VMEM((2, 7, nh // 2, 8, nv), jnp.float32),
                pltpu.VMEM((2, nx, ny, nv), jnp.float32),
                pltpu.VMEM((8, 128), jnp.float32),
                pltpu.VMEM((n_xy - 1, 8, 128), jnp.float32),
                pltpu.VMEM((8, nv), jnp.float32),
                pltpu.SemaphoreType.DMA((3, count)),
                pltpu.SemaphoreType.DMA((3, count)),
                pltpu.SemaphoreType.DMA((n_xy - 1,)),
                pltpu.SemaphoreType.DMA((n_xy - 1,)),
                pltpu.SemaphoreType.DMA((tiles, len(head_chunks(nh)))),
            ],
            compiler_params=pltpu.CompilerParams(
                collective_id=0, has_side_effects=True, vmem_limit_bytes=56 * 2**20
            ),
        )(level_set.transpose(0, 2, 1, 3), wind_field, jnp.asarray(flow), jnp.asarray(ends))
        return increment.transpose(0, 2, 1, 3)

    return jax.shard_map(
        body,
        mesh=mesh,
        in_specs=(P("gx", "gy", "ha", None), P(None, "gx", "gy")),
        out_specs=P("gx", "gy", "ha", None),
        check_vma=False,
    )
```

time: 51.5 us -> 45 us (0.87)
  Pallas kernels: 49.4 us -> 42.8 us
    pallas_call x1, Pallas kernels: 49.4 us -> 42.8 us  [body(): pl.pallas_call(functools.partial(kernel, (nx, ny, nh, nv), axes), out_sha...]
where the time goes in v1:
time: 45 us; the launch traced here: 44.8 us
  Pallas kernels  42.8 us (95%)
  local copies, waits for them, and re-layouts  1.97 us (4%)
    pallas_call x1, Pallas kernels, body(): pl.pallas_call(functools.partial(kernel, (nx, ny, nh, nv), axes), out_sha...  42.8 us
    unnamed x1, local copies, waits for them, and re-layouts  1.97 us

profile of v1, /device:TPU:0, one launch (start us, length us, event | category | flops | bytes accessed | tf_op | source)
XLA Modules:
  0.0 44.8 jit_solution(17763177925095178032)
XLA Ops:
  0.0 42.8 %shard_map.46 = f32[8,10,16,128]{3,2,1,0:T(8,128)} custom-call(f32[8,10,16,128]{3,2,1,0:T(8,128)} %bitcast.3, f32[2,8,16]{2,1,0:T(8,128)} %wind_ref.1, f32[2,40,128]{2,1,0:T(8,128)} %constant.4.clone.flow_ref, f32[2,1,128]{2,1,0:T(1,128)} %constant.5.clone.rate_ref), custom_call_target="tpu_custom_call" | custom-call | tf_op jit(solution)/shard_map/pallas_call | solution.py:484
  42.9 2.0 %copy.6 = f32[8,16,10,128]{3,1,2,0:T(8,128)} copy(f32[8,16,10,128]{3,1,2,0:T(8,128)} %bitcast.2) | data formatting | bytes 1310720

commit v2 on v1

--- a/solution.py
+++ b/solution.py
@@ -86,7 +86,15 @@
 
 
 def head_chunks(nh):
-    return ((0, 3), (nh - 3, 3), (3, nh - 6))
+    half = (nh - 6) // 2
+    return ((0, 3), (nh - 3, 3), (3, half), (3 + half, nh - 6 - half))
+
+
+RELAYED = (0, 2)
+
+
+def folded(axes):
+    return axes[0] == 4 and axes[1] == 2
 
 
 def plane_chunks(nx):
@@ -99,8 +107,8 @@
 
 
 def kernel(sizes, axes, u_ref, wind_ref, flow_ref, rate_ref, out_hbm,
-           b0, b1, b2, acc, rights, out_ref, va, vb, wind, best, peers, step,
-           sends, recvs, rsend, rrecv, osem):
+           b0, b1, b2, acc, rights, out_ref, va, vb, wind, best, peers, step, relay,
+           sends, recvs, rsend, rrecv, osem, lsend, lrecv):
     nx, ny, nh, nv = sizes
     ngx, ngy, nha = axes
     bufs = (b0, b1, b2)
@@ -149,6 +157,9 @@
 
     def tile_rows(t):
         return pl.ds(PAD + 8 * t, 8)
+
+    bending = folded(axes)
+    places = []
 
     def copies(s):
         buf = bufs[s]
@@ -163,11 +174,12 @@
                 )
             for c, (k0, count) in enumerate(heads):
                 hc = pl.ds(3 + k0, count)
+                around = bending and c in RELAYED
                 plans["x", t, c] = (
                     (buf.at[pl.ds(nx, 3), hc, ys], buf.at[pl.ds(0, 3), hc, ys], {"gx": gx + 1},
-                     gx < ngx - 1, gx > 0),
+                     (gx == 0) | (gx == 2) if around else gx < ngx - 1, gx > 0),
                     (buf.at[pl.ds(3, 3), hc, ys], buf.at[pl.ds(3 + nx, 3), hc, ys], {"gx": gx - 1},
-                     gx > 0, gx < ngx - 1),
+                     (gx == 1) | (gx == 3) if around else gx > 0, gx < ngx - 1),
                 )
         xs = pl.ds(3, nx)
         for c, (k0, count) in enumerate(heads):
@@ -180,15 +192,17 @@
                 (buf.at[xs, hc, pl.ds(PAD, PAD)], buf.at[xs, hc, pl.ds(PAD + ny, PAD)], {"gy": gy - 1},
                  gy > 0, gy < ngy - 1),
             )
-        made, at = {}, 0
+        made, at, starts = {}, 0, {}
         for key, group_of in plans.items():
             row = []
+            starts[key] = at
             for src, dst, target, has_out, has_in in group_of:
                 row.append((pltpu.make_async_remote_copy(
                     src_ref=src, dst_ref=dst, send_sem=sends.at[s, at], recv_sem=recvs.at[s, at],
                     device_id=target, device_id_type=MESH), has_out, has_in))
                 at += 1
             made[key] = row
+        places.append(starts)
         return made
 
     def under(condition, act):
@@ -205,7 +219,45 @@
     ]
     plans = [copies(s) for s in range(3)]
 
+    built = {}
+
+    def legs(s, t, c):
+        if (s, t, c) in built:
+            return built[s, t, c]
+        buf = bufs[s]
+        k0, count = heads[c]
+        hc, ys = pl.ds(3 + k0, count), tile_rows(t)
+        held = relay.at[s, pl.ds(0, 3), pl.ds(k0, count), pl.ds(8 * t, 8)]
+        i = RELAYED.index(c)
+        rows = []
+        for way, (src, dst, origin, middle, end) in enumerate((
+            (buf.at[pl.ds(nx, 3), hc, ys], buf.at[pl.ds(0, 3), hc, ys], 1, 3, 2),
+            (buf.at[pl.ds(3, 3), hc, ys], buf.at[pl.ds(3 + nx, 3), hc, ys], 2, 0, 1),
+        )):
+            out = pltpu.make_async_remote_copy(
+                src_ref=src, dst_ref=held, send_sem=lsend.at[s, t, i, way], recv_sem=lrecv.at[s, t, i, way],
+                device_id={"gx": middle}, device_id_type=MESH)
+            on = pltpu.make_async_remote_copy(
+                src_ref=held, dst_ref=dst, send_sem=sends.at[s, places[s]["x", t, c] + way],
+                recv_sem=recvs.at[s, places[s]["x", t, c] + way],
+                device_id={"gx": end}, device_id_type=MESH)
+            rows.append((out, on, gx == origin, gx == middle))
+        built[s, t, c] = rows
+        return rows
+
+    def forward(s, t):
+        if bending:
+            for c in RELAYED:
+                for out, on, _, here in legs(s, t, c):
+                    @pl.when(here)
+                    def _():
+                        out.wait_recv()
+                        on.start()
+
     def send(s, *key):
+        if bending and key[0] == "x" and key[2] in RELAYED:
+            for out, _, from_here, _ in legs(s, *key[1:]):
+                under(from_here, out.start)
         for copy, has_out, _ in plans[s].get(key, ()):
             under(has_out, copy.start)
 
@@ -431,7 +483,10 @@
         y_pass(s, 0)
         for t in range(1, tiles):
             v_pass(bufs[s], t)
+            if s == 0:
+                forward(s, t - 1)
             y_pass(s, t)
+        forward(s, tiles - 1)
         for t in range(tiles):
             fill_x(bufs[s], t)
             h_pass(s, t)
@@ -446,6 +501,8 @@
             x_pass(s, t)
             if s < 2 and t == 0:
                 v_pass(bufs[s + 1], 0)
+            if s < 2 and t > 0:
+                forward(s + 1, t - 1)
 
     for t in range(tiles):
         for c in range(len(heads)):
@@ -456,6 +513,12 @@
         for row in plans[s].values():
             for copy, has_out, _ in row:
                 under(has_out, copy.wait_send)
+        if bending:
+            for t in range(tiles):
+                for c in RELAYED:
+                    for out, on, from_here, here in legs(s, t, c):
+                        under(from_here, out.wait_send)
+                        under(here, on.wait_send)
 
 
 def tables(nv, n_head):
@@ -494,11 +557,14 @@
                 pltpu.VMEM((8, 128), jnp.float32),
                 pltpu.VMEM((n_xy - 1, 8, 128), jnp.float32),
                 pltpu.VMEM((8, nv), jnp.float32),
+                pltpu.VMEM((3, 3, nh, ny, nv), jnp.float32),
                 pltpu.SemaphoreType.DMA((3, count)),
                 pltpu.SemaphoreType.DMA((3, count)),
                 pltpu.SemaphoreType.DMA((n_xy - 1,)),
                 pltpu.SemaphoreType.DMA((n_xy - 1,)),
                 pltpu.SemaphoreType.DMA((tiles, len(head_chunks(nh)))),
+                pltpu.SemaphoreType.DMA((3, tiles, len(RELAYED), 2)),
+                pltpu.SemaphoreType.DMA((3, tiles, len(RELAYED), 2)),
             ],
             compiler_params=pltpu.CompilerParams(
                 collective_id=0, has_side_effects=True, vmem_limit_bytes=56 * 2**20

time: 45 us -> 40.8 us (0.907)
  Pallas kernels: 42.8 us -> 38.3 us
    pallas_call x1, Pallas kernels: 42.8 us -> 38.3 us  [body(): pl.pallas_call(functools.partial(kernel, (nx, ny, nh, nv), axes), out_sha...]
where the time goes in v2:
time: 40.8 us; the launch traced here: 40.3 us
  Pallas kernels  38.3 us (94%)
  local copies, waits for them, and re-layouts  1.97 us (5%)
    pallas_call x1, Pallas kernels, body(): pl.pallas_call(functools.partial(kernel, (nx, ny, nh, nv), axes), out_sha...  38.3 us
    unnamed x1, local copies, waits for them, and re-layouts  1.97 us

profile of v2, /device:TPU:0, one launch (start us, length us, event | category | flops | bytes accessed | tf_op | source)
XLA Modules:
  0.0 40.3 jit_solution(1641689190034109879)
XLA Ops:
  0.0 38.3 %shard_map.46 = f32[8,10,16,128]{3,2,1,0:T(8,128)} custom-call(f32[8,10,16,128]{3,2,1,0:T(8,128)} %bitcast.3, f32[2,8,16]{2,1,0:T(8,128)} %wind_ref.1, f32[2,40,128]{2,1,0:T(8,128)} %constant.4.clone.flow_ref, f32[2,1,128]{2,1,0:T(1,128)} %constant.5.clone.rate_ref), custom_call_target="tpu_custom_call" | custom-call | tf_op jit(solution)/shard_map/pallas_call | solution.py:547
  38.3 2.0 %copy.6 = f32[8,16,10,128]{3,1,2,0:T(8,128)} copy(f32[8,16,10,128]{3,1,2,0:T(8,128)} %bitcast.2) | data formatting | bytes 1310720

commit v3 on v2

--- a/solution.py
+++ b/solution.py
@@ -94,7 +94,7 @@
 
 
 def folded(axes):
-    return axes[0] == 4 and axes[1] == 2
+    return axes[0] == 4 and axes[1] == 2 and axes[2] > 2
 
 
 def plane_chunks(nx):
@@ -106,9 +106,9 @@
     return 2 * tiles * len(plane_chunks(nx)) + 2 * len(head_chunks(nh)) * (tiles + 1)
 
 
-def kernel(sizes, axes, u_ref, wind_ref, flow_ref, rate_ref, out_hbm,
-           b0, b1, b2, acc, rights, out_ref, va, vb, wind, best, peers, step, relay,
-           sends, recvs, rsend, rrecv, osem, lsend, lrecv):
+def kernel(sizes, axes, u_hbm, wind_hbm, flow_hbm, rate_hbm, out_ref,
+           b0, b1, b2, acc, rights, u_ref, wind_ref, flow_ref, rate_ref, va, vb, wind, best, peers, step, relay,
+           sends, recvs, rsend, rrecv, isem, lsend, lrecv, far_x, low_in, high_in):
     nx, ny, nh, nv = sizes
     ngx, ngy, nha = axes
     bufs = (b0, b1, b2)
@@ -127,11 +127,44 @@
 
     up_ha = {"ha": lax.rem(ha + 1, nha)}
     down_ha = {"ha": lax.rem(ha + nha - 1, nha)}
+    bending = folded(axes)
+    beside, across = gx + 1 - 2 * lax.rem(gx, 2), lax.rem(gx + 2, 4)
+    near = ({"gy": 1 - gy}, {"gx": beside}, {"gx": across},
+            {"gx": beside, "gy": 1 - gy}, {"gx": across, "gy": 1 - gy})
+
+    def under(condition, act):
+        if condition is None:
+            act()
+        else:
+            pl.when(condition)(act)
+
+    def signal(semaphore, target):
+        return lambda: pl.semaphore_signal(semaphore, inc=1, device_id=target, device_id_type=MESH)
+
+    def await_one(semaphore):
+        return lambda: pl.semaphore_wait(semaphore, 1)
+
     barrier = pltpu.get_barrier_semaphore()
-    for delta in range(1, n_xy):
-        pl.semaphore_signal(barrier, inc=1, device_id=peer(delta), device_id_type=MESH)
-    for target in (up_ha, down_ha):
-        pl.semaphore_signal(barrier, inc=1, device_id=target, device_id_type=MESH)
+    if bending:
+        for target in near:
+            signal(barrier, target)()
+        under(ha < nha - 1, signal(barrier, {"ha": ha + 1}))
+        under(ha > 0, signal(barrier, {"ha": ha - 1}))
+    else:
+        for delta in range(1, n_xy):
+            signal(barrier, peer(delta))()
+        for target in (up_ha, down_ha):
+            signal(barrier, target)()
+
+    fetches = [
+        pltpu.make_async_copy(src, dst, isem.at[i])
+        for i, (src, dst) in enumerate((
+            (wind_hbm, wind_ref), (rate_hbm, rate_ref), (u_hbm, u_ref), (flow_hbm, flow_ref)))
+    ]
+    for fetch in fetches:
+        fetch.start()
+    for fetch in fetches:
+        fetch.wait()
 
     def load_plane(x, carry):
         for k in range(nh):
@@ -153,12 +186,15 @@
 
     best[...] = lax.fori_loop(0, nx, rate_plane, jnp.zeros((8, 128), jnp.float32))
 
-    pl.semaphore_wait(barrier, n_xy + 1)
+    if bending:
+        beyond = (ha + nha - 2) // (nha - 1) + (2 * nha - 3 - ha) // (nha - 1)
+        pl.semaphore_wait(barrier, len(near) + beyond)
+    else:
+        pl.semaphore_wait(barrier, n_xy + 1)
 
     def tile_rows(t):
         return pl.ds(PAD + 8 * t, 8)
 
-    bending = folded(axes)
     places = []
 
     def copies(s):
@@ -205,18 +241,21 @@
         places.append(starts)
         return made
 
-    def under(condition, act):
-        if condition is None:
-            act()
-        else:
-            pl.when(condition)(act)
-
     rate_copies = [
         pltpu.make_async_remote_copy(
             src_ref=best, dst_ref=peers.at[delta - 1], send_sem=rsend.at[delta - 1],
             recv_sem=rrecv.at[delta - 1], device_id=peer(delta), device_id_type=MESH)
         for delta in range(1, n_xy)
     ]
+
+    def settle_rate():
+        top = best[...]
+        for i, copy in enumerate(rate_copies):
+            copy.wait_recv()
+            top = jnp.maximum(top, peers[i])
+        rate = jnp.max(top, axis=(0, 1), keepdims=True) + (TURN_MAX / d_theta + ACCEL_MAX / d_speed)
+        step[...] = jnp.broadcast_to(CFL_NUMBER / rate, step.shape)
+
     plans = [copies(s) for s in range(3)]
 
     built = {}
@@ -390,11 +429,6 @@
                     under(has_in, copy.wait_recv)
         lax.fori_loop(0, nx, body, 0)
 
-    def out_copy(t, c):
-        k0, count = heads[c]
-        part = (pl.ds(0, nx), pl.ds(k0, count), pl.ds(8 * t, 8))
-        return pltpu.make_async_copy(out_ref.at[part], out_hbm.at[part], osem.at[t, c])
-
     def x_pass(s, t):
         buf = bufs[s]
         eps = eps_of(CELL_SIZE)
@@ -427,8 +461,6 @@
                 if c == 1:
                     for p in range(len(planes)):
                         send(s + 1, "h", t, p)
-            else:
-                out_copy(t, c).start()
 
     def fill_x(buf, t):
         rows = tile_rows(t)
@@ -467,16 +499,69 @@
         if t == tiles - 1:
             pl.when(gy == ngy - 1)(ends(False))
 
-    for t in range(tiles):
+    def open_x(t, far):
+        for c in range(len(heads)):
+            if far and c in RELAYED:
+                continue
+            for way, (copy, _, _) in enumerate(plans[0]["x", t, c]):
+                under(gx == 1 + way if far else lax.rem(gx, 2) == way, copy.start)
+            if c in RELAYED:
+                for out, _, from_here, _ in legs(0, t, c):
+                    under(from_here, out.start)
+
+    def open_h(t, far):
         for p in range(len(planes)):
-            send(0, "h", t, p)
+            for way, (copy, _, _) in enumerate(plans[0]["h", t, p]):
+                edge = (nha - 1) * (1 - way)
+                under(ha == edge if far else ha != edge, copy.start)
+
+    def open_y(t):
         for c in range(len(heads)):
-            send(0, "x", t, c)
             send(0, "y", t, c)
-        if t == 0:
-            for copy in rate_copies:
-                copy.start()
-    v_pass(b0, 0)
+
+    if bending:
+        open_h(0, False)
+        open_x(0, False)
+        open_y(tiles - 1)
+        signal(far_x, {"gx": beside})()
+        under(ha == 1, signal(low_in, {"ha": ha + 1}))
+        under(ha == nha - 2, signal(high_in, {"ha": ha - 1}))
+        open_y(0) if tiles > 1 else None
+
+        @pl.when((ha > 1) & (ha < nha - 1))
+        def _():
+            await_one(low_in)()
+            signal(low_in, {"ha": ha + 1})()
+
+        @pl.when((ha > 0) & (ha < nha - 2))
+        def _():
+            await_one(high_in)()
+            signal(high_in, {"ha": ha - 1})()
+
+        await_one(far_x)()
+        open_x(0, True)
+        for copy in rate_copies:
+            copy.start()
+        for t in range(1, tiles):
+            open_x(t, False)
+            open_x(t, True)
+        v_pass(b0, 0)
+        under(ha == nha - 1, await_one(low_in))
+        under(ha == 0, await_one(high_in))
+        open_h(0, True)
+        for t in range(1, tiles):
+            open_h(t, False)
+            open_h(t, True)
+    else:
+        for t in range(tiles):
+            for p in range(len(planes)):
+                send(0, "h", t, p)
+            for c in range(len(heads)):
+                send(0, "x", t, c)
+                send(0, "y", t, c)
+        for copy in rate_copies:
+            copy.start()
+        v_pass(b0, 0)
     for s in range(3):
         fill_y(bufs[s], 0)
         fill_y(bufs[s], tiles - 1) if tiles > 1 else None
@@ -491,22 +576,13 @@
             fill_x(bufs[s], t)
             h_pass(s, t)
             if s == 0 and t == 0:
-                for copy in rate_copies:
-                    copy.wait_recv()
-                top = best[...]
-                for delta in range(1, n_xy):
-                    top = jnp.maximum(top, peers[delta - 1])
-                rate = jnp.max(top, axis=(0, 1), keepdims=True) + (TURN_MAX / d_theta + ACCEL_MAX / d_speed)
-                step[...] = jnp.broadcast_to(CFL_NUMBER / rate, step.shape)
+                settle_rate()
             x_pass(s, t)
             if s < 2 and t == 0:
                 v_pass(bufs[s + 1], 0)
             if s < 2 and t > 0:
                 forward(s + 1, t - 1)
 
-    for t in range(tiles):
-        for c in range(len(heads)):
-            out_copy(t, c).wait()
     for copy in rate_copies:
         copy.wait_send()
     for s in range(3):
@@ -546,11 +622,14 @@
         vmem = pl.BlockSpec(memory_space=pltpu.VMEM)
         increment = pl.pallas_call(
             functools.partial(kernel, (nx, ny, nh, nv), axes),
-            out_shape=jax.ShapeDtypeStruct((nx, nh, ny, nv), jnp.float32),
-            in_specs=[vmem, pl.BlockSpec(memory_space=pltpu.SMEM), vmem, vmem],
-            out_specs=pl.BlockSpec(memory_space=pltpu.HBM),
+            out_shape=pltpu.VMEM((nx, nh, ny, nv), jnp.float32),
+            in_specs=[pl.BlockSpec(memory_space=pltpu.HBM)] * 4,
+            out_specs=vmem,
             scratch_shapes=[
                 state, state, state, cells, cells, cells,
+                pltpu.SMEM((2, nx, ny), jnp.float32),
+                pltpu.VMEM(flow.shape, jnp.float32),
+                pltpu.VMEM(ends.shape, jnp.float32),
                 pltpu.VMEM((2, 2, nh // 2, 8, nv), jnp.float32),
                 pltpu.VMEM((2, 7, nh // 2, 8, nv), jnp.float32),
                 pltpu.VMEM((2, nx, ny, nv), jnp.float32),
@@ -562,9 +641,12 @@
                 pltpu.SemaphoreType.DMA((3, count)),
                 pltpu.SemaphoreType.DMA((n_xy - 1,)),
                 pltpu.SemaphoreType.DMA((n_xy - 1,)),
-                pltpu.SemaphoreType.DMA((tiles, len(head_chunks(nh)))),
+                pltpu.SemaphoreType.DMA((4,)),
                 pltpu.SemaphoreType.DMA((3, tiles, len(RELAYED), 2)),
                 pltpu.SemaphoreType.DMA((3, tiles, len(RELAYED), 2)),
+                pltpu.SemaphoreType.REGULAR,
+                pltpu.SemaphoreType.REGULAR,
+                pltpu.SemaphoreType.REGULAR,
             ],
             compiler_params=pltpu.CompilerParams(
                 collective_id=0, has_side_effects=True, vmem_limit_bytes=56 * 2**20

time: 40.8 us -> 38.1 us (0.934)
  Pallas kernels: 38.3 us -> 36.9 us
  local copies, waits for them, and re-layouts: 1.97 us -> 0.84 us
    pallas_call x1, Pallas kernels: 38.3 us -> 36.9 us  [body(): pl.pallas_call(functools.partial(kernel, (nx, ny, nh, nv), axes), out_sha...]
    unnamed x1, local copies, waits for them, and re-layouts: 1.97 us -> 0.84 us
where the time goes in v3:
time: 38.1 us; the launch traced here: 37.7 us
  Pallas kernels  36.9 us (97%)
  local copies, waits for them, and re-layouts  0.84 us (2%)
    pallas_call x1, Pallas kernels, body(): pl.pallas_call(functools.partial(kernel, (nx, ny, nh, nv), axes), out_sha...  36.9 us
    unnamed x1, local copies, waits for them, and re-layouts  0.84 us

profile of v3, /device:TPU:0, one launch (start us, length us, event | category | flops | bytes accessed | tf_op | source)
XLA Modules:
  0.0 37.7 jit_solution(8306108949664124150)
XLA Ops:
  0.0 36.9 %shard_map.46 = f32[8,10,16,128]{3,2,1,0:T(8,128)S(1)} custom-call(f32[8,10,16,128]{3,2,1,0:T(8,128)} %bitcast.3, f32[2,8,16]{2,1,0:T(8,128)} %wind_hbm.1, f32[2,40,128]{2,1,0:T(8,128)} %constant.4.clone.flow_hbm, f32[2,1,128]{2,1,0:T(1,128)} %constant.5.clone.rate_hbm), custom_call_target="tpu_custom_call" | custom-call | tf_op jit(solution)/shard_map/pallas_call | solution.py:623
  36.9 0.8 %copy.6 = f32[8,16,10,128]{3,1,2,0:T(8,128)} copy(f32[8,16,10,128]{3,1,2,0:T(8,128)S(1)} %bitcast.2) | data formatting | bytes 1310720

commit v4 on v3

--- a/solution.py
+++ b/solution.py
@@ -86,11 +86,11 @@
 
 
 def head_chunks(nh):
-    half = (nh - 6) // 2
-    return ((0, 3), (nh - 3, 3), (3, half), (3 + half, nh - 6 - half))
-
-
-RELAYED = (0, 2)
+    half = nh // 2
+    return ((0, half), (half, nh - half))
+
+
+RELAYED = (1,)
 
 
 def folded(axes):
@@ -103,7 +103,7 @@
 
 
 def n_copies(nx, nh, tiles):
-    return 2 * tiles * len(plane_chunks(nx)) + 2 * len(head_chunks(nh)) * (tiles + 1)
+    return 2 * len(plane_chunks(nx)) * (tiles + 1) + 2 * len(head_chunks(nh)) * tiles
 
 
 def kernel(sizes, axes, u_hbm, wind_hbm, flow_hbm, rate_hbm, out_ref,
@@ -217,9 +217,9 @@
                     (buf.at[pl.ds(3, 3), hc, ys], buf.at[pl.ds(3 + nx, 3), hc, ys], {"gx": gx - 1},
                      (gx == 1) | (gx == 3) if around else gx > 0, gx < ngx - 1),
                 )
-        xs = pl.ds(3, nx)
-        for c, (k0, count) in enumerate(heads):
-            hc = pl.ds(3 + k0, count)
+        hc = pl.ds(3, nh)
+        for c, (x0, count) in enumerate(planes):
+            xs = pl.ds(3 + x0, count)
             plans["y", tiles - 1, c] = (
                 (buf.at[xs, hc, pl.ds(ny, PAD)], buf.at[xs, hc, pl.ds(0, PAD)], {"gy": gy + 1},
                  gy < ngy - 1, gy > 0),
@@ -294,17 +294,22 @@
                         on.start()
 
     def send(s, *key):
-        if bending and key[0] == "x" and key[2] in RELAYED:
-            for out, _, from_here, _ in legs(s, *key[1:]):
-                under(from_here, out.start)
         for copy, has_out, _ in plans[s].get(key, ()):
             under(has_out, copy.start)
+
+    def send_x(s, t, way):
+        for c in range(len(heads)):
+            copy, has_out, _ = plans[s]["x", t, c][way]
+            under(has_out, copy.start)
+            if bending and c in RELAYED:
+                out, _, from_here, _ = legs(s, t, c)[way]
+                under(from_here, out.start)
 
     def wait_in(s, *key):
         for copy, _, has_in in plans[s].get(key, ()):
             under(has_in, copy.wait_recv)
 
-    def v_pass(buf, t):
+    def v_parts(buf, t):
         eps = eps_of(d_speed)
         coef = ACCEL_MAX / (3.0 * d_speed)
         e4 = np.float32(np.float32(eps * eps) ** 2)
@@ -361,9 +366,10 @@
                 acc[x, k, rows_acc, :] = coef * left
                 rights[x, k, rows_acc, :] = coef * right
 
-        first(0, 0)
-        first(0, 1)
-        second(0)
+        def begin():
+            first(0, 0)
+            first(0, 1)
+            second(0)
 
         def body(x, carry):
             after = jnp.minimum(x + 1, nx - 1)
@@ -375,6 +381,11 @@
             first(after, 1)
             return carry
 
+        return begin, body
+
+    def v_pass(buf, t):
+        begin, body = v_parts(buf, t)
+        begin()
         lax.fori_loop(0, nx, body, 0)
 
     def h_pass(s, t):
@@ -384,6 +395,7 @@
         rows, rows_acc = tile_rows(t), pl.ds(8 * t, 8)
 
         def body(x, carry):
+            dt = step[...]
             u = [buf[3 + x, j, rows, :] for j in range(nh + 6)]
             q = [u[j + 1] - u[j] for j in range(nh + 5)]
             d = [q[j + 1] - q[j] for j in range(nh + 4)]
@@ -394,21 +406,45 @@
                     q[f + 2], d[f + 1], d[f + 2], tr[f][0], tr[f + 1][0], tr[f + 2][0],
                     tr[f][1], tr[f + 1][2], tr[f + 2][3])
                 if before is not None:
-                    acc[x, f - 1, rows_acc, :] += coef * jnp.minimum(before, right)
+                    k = f - 1
+                    total = acc[x, k, rows_acc, :] + coef * jnp.minimum(before, right)
+                    moved = u[k + 3] - dt * jnp.maximum(total, 0.0)
+                    if s == 0:
+                        b1[3 + x, 3 + k, rows, :] = moved
+                    elif s == 1:
+                        b2[3 + x, 3 + k, rows, :] = 0.75 * b0[3 + x, 3 + k, rows, :] + 0.25 * moved
+                    else:
+                        out_ref[x, k, rows_acc, :] = (moved - b0[3 + x, 3 + k, rows, :]) * (2.0 / (3.0 * SCALE))
                 before = left
             return carry
 
         for c, (x0, count) in enumerate(planes):
             wait_in(s, "h", t, c)
             lax.fori_loop(x0, x0 + count, body, 0)
+            if s < 2:
+                send(s + 1, "h", t, c)
+                if c == 0:
+                    send_x(s + 1, t, 1)
+                if c == len(planes) - 1:
+                    send_x(s + 1, t, 0)
+                send(s + 1, "y", t, c)
 
     def flow_row(comp, k):
         return flow_ref[comp, pl.ds(ha * nh + k, 1), :]
 
-    def y_pass(s, t):
+    def y_parts(s, t):
         buf = bufs[s]
         eps = eps_of(CELL_SIZE)
         rows = slice(8 * t, 8 * t + 8)
+
+        def begin():
+            for c in range(len(planes)):
+                if t == 0:
+                    for copy, _, has_in in plans[s]["y", tiles - 1, c][:1]:
+                        under(has_in, copy.wait_recv)
+                if t == tiles - 1:
+                    for copy, _, has_in in plans[s]["y", 0, c][-1:]:
+                        under(has_in, copy.wait_recv)
 
         def body(x, carry):
             for k in range(nh):
@@ -420,13 +456,24 @@
                 acc[x, k, rows, :] = along_v + upwind(*d, q[2], q[3], fh, eps)
             return carry
 
-        for c in range(len(heads)):
-            if t == 0:
-                for copy, _, has_in in plans[s]["y", tiles - 1, c][:1]:
-                    under(has_in, copy.wait_recv)
-            if t == tiles - 1:
-                for copy, _, has_in in plans[s]["y", 0, c][-1:]:
-                    under(has_in, copy.wait_recv)
+        return begin, body
+
+    def y_pass(s, t):
+        begin, body = y_parts(s, t)
+        begin()
+        lax.fori_loop(0, nx, body, 0)
+
+    def yv_pass(s, t):
+        y_begin, y_body = y_parts(s, t)
+        v_begin, v_body = v_parts(bufs[s], t + 1)
+        v_begin()
+        y_begin()
+
+        def body(x, carry):
+            y_body(x, carry)
+            v_body(x, carry)
+            return carry
+
         lax.fori_loop(0, nx, body, 0)
 
     def x_pass(s, t):
@@ -436,31 +483,17 @@
 
         def body(k, carry):
             row = flow_row(0, k)
-            dt = step[...]
             u = [buf[j, 3 + k, rows, :] for j in range(nx + 6)]
             q = [u[j + 1] - u[j] for j in range(nx + 5)]
             d = [q[j + 1] - q[j] for j in range(nx + 4)]
             for x in range(nx):
                 fh = row + wind[0, x, rows_acc, :]
-                total = acc[x, k, rows_acc, :] + upwind(*d[x:x + 5], q[x + 2], q[x + 3], fh, eps)
-                moved = u[x + 3] - dt * jnp.maximum(total, 0.0)
-                if s == 0:
-                    b1[3 + x, 3 + k, rows, :] = moved
-                elif s == 1:
-                    b2[3 + x, 3 + k, rows, :] = 0.75 * b0[3 + x, 3 + k, rows, :] + 0.25 * moved
-                else:
-                    out_ref[x, k, rows_acc, :] = (moved - b0[3 + x, 3 + k, rows, :]) * (2.0 / (3.0 * SCALE))
+                acc[x, k, rows_acc, :] += upwind(*d[x:x + 5], q[x + 2], q[x + 3], fh, eps)
             return carry
 
         for c, (k0, count) in enumerate(heads):
             wait_in(s, "x", t, c)
             lax.fori_loop(k0, k0 + count, body, 0)
-            if s < 2:
-                send(s + 1, "x", t, c)
-                send(s + 1, "y", t, c)
-                if c == 1:
-                    for p in range(len(planes)):
-                        send(s + 1, "h", t, p)
 
     def fill_x(buf, t):
         rows = tile_rows(t)
@@ -516,8 +549,16 @@
                 under(ha == edge if far else ha != edge, copy.start)
 
     def open_y(t):
-        for c in range(len(heads)):
+        for c in range(len(planes)):
             send(0, "y", t, c)
+
+    def open_tile(t, along_x=True, along_h=True):
+        if bending and along_x:
+            open_x(t, False)
+            open_x(t, True)
+        if bending and along_h:
+            open_h(t, False)
+            open_h(t, True)
 
     if bending:
         open_h(0, False)
@@ -542,46 +583,40 @@
         open_x(0, True)
         for copy in rate_copies:
             copy.start()
-        for t in range(1, tiles):
-            open_x(t, False)
-            open_x(t, True)
         v_pass(b0, 0)
         under(ha == nha - 1, await_one(low_in))
         under(ha == 0, await_one(high_in))
         open_h(0, True)
-        for t in range(1, tiles):
-            open_h(t, False)
-            open_h(t, True)
     else:
         for t in range(tiles):
             for p in range(len(planes)):
                 send(0, "h", t, p)
-            for c in range(len(heads)):
-                send(0, "x", t, c)
-                send(0, "y", t, c)
+                send(0, "y", t, p)
+            for way in range(2):
+                send_x(0, t, way)
         for copy in rate_copies:
             copy.start()
         v_pass(b0, 0)
     for s in range(3):
         fill_y(bufs[s], 0)
         fill_y(bufs[s], tiles - 1) if tiles > 1 else None
-        y_pass(s, 0)
         for t in range(1, tiles):
-            v_pass(bufs[s], t)
+            yv_pass(s, t - 1)
             if s == 0:
                 forward(s, t - 1)
-            y_pass(s, t)
+                open_tile(t)
+        y_pass(s, tiles - 1)
         forward(s, tiles - 1)
         for t in range(tiles):
             fill_x(bufs[s], t)
-            h_pass(s, t)
+            x_pass(s, t)
             if s == 0 and t == 0:
                 settle_rate()
-            x_pass(s, t)
+            if s < 2 and t > 0:
+                forward(s + 1, t - 1)
+            h_pass(s, t)
             if s < 2 and t == 0:
                 v_pass(bufs[s + 1], 0)
-            if s < 2 and t > 0:
-                forward(s + 1, t - 1)
 
     for copy in rate_copies:
         copy.wait_send()

time: 38.1 us -> 36.6 us (0.961)
  Pallas kernels: 36.9 us -> 35.6 us
    pallas_call x1, Pallas kernels: 36.9 us -> 35.6 us  [body(): pl.pallas_call(functools.partial(kernel, (nx, ny, nh, nv), axes), out_sha...]
where the time goes in v4:
time: 36.6 us; the launch traced here: 36.4 us
  Pallas kernels  35.6 us (97%)
  local copies, waits for them, and re-layouts  0.84 us (2%)
    pallas_call x1, Pallas kernels, body(): pl.pallas_call(functools.partial(kernel, (nx, ny, nh, nv), axes), out_sha...  35.6 us
    unnamed x1, local copies, waits for them, and re-layouts  0.84 us

profile of v4, /device:TPU:0, one launch (start us, length us, event | category | flops | bytes accessed | tf_op | source)
XLA Modules:
  0.0 36.4 jit_solution(17898886662375081154)
XLA Ops:
  0.0 35.6 %shard_map.46 = f32[8,10,16,128]{3,2,1,0:T(8,128)S(1)} custom-call(f32[8,10,16,128]{3,2,1,0:T(8,128)} %bitcast.3, f32[2,8,16]{2,1,0:T(8,128)} %wind_hbm.1, f32[2,40,128]{2,1,0:T(8,128)} %constant.4.clone.flow_hbm, f32[2,1,128]{2,1,0:T(1,128)} %constant.5.clone.rate_hbm), custom_call_target="tpu_custom_call" | custom-call | tf_op jit(solution)/shard_map/pallas_call | solution.py:658
  35.6 0.8 %copy.6 = f32[8,16,10,128]{3,1,2,0:T(8,128)} copy(f32[8,16,10,128]{3,1,2,0:T(8,128)S(1)} %bitcast.2) | data formatting | bytes 1310720

commit v5 on v4

--- a/solution.py
+++ b/solution.py
@@ -557,7 +557,9 @@
             open_x(t, False)
             open_x(t, True)
         if bending and along_h:
-            open_h(t, False)
+            for p in range(1, len(planes)):
+                for way, (copy, _, _) in enumerate(plans[0]["h", t, p]):
+                    under(ha != (nha - 1) * (1 - way), copy.start)
             open_h(t, True)
 
     if bending:
@@ -581,6 +583,9 @@
 
         await_one(far_x)()
         open_x(0, True)
+        for t in range(1, tiles):
+            for way, (copy, _, _) in enumerate(plans[0]["h", t, 0]):
+                under(ha != (nha - 1) * (1 - way), copy.start)
         for copy in rate_copies:
             copy.start()
         v_pass(b0, 0)
@@ -606,10 +611,13 @@
                 forward(s, t - 1)
                 open_tile(t)
         y_pass(s, tiles - 1)
-        forward(s, tiles - 1)
+        if tiles == 1:
+            forward(s, 0)
         for t in range(tiles):
             fill_x(bufs[s], t)
             x_pass(s, t)
+            if t == 0 and tiles > 1:
+                forward(s, tiles - 1)
             if s == 0 and t == 0:
                 settle_rate()
             if s < 2 and t > 0:

time: 36.6 us -> 36.3 us (level)
  Pallas kernels: 35.6 us -> 35.2 us
where the time goes in v5:
time: 36.3 us; the launch traced here: 36.1 us
  Pallas kernels  35.2 us (97%)
  local copies, waits for them, and re-layouts  0.84 us (2%)
    pallas_call x1, Pallas kernels, body(): pl.pallas_call(functools.partial(kernel, (nx, ny, nh, nv), axes), out_sha...  35.2 us
    unnamed x1, local copies, waits for them, and re-layouts  0.84 us

profile of v5, /device:TPU:0, one launch (start us, length us, event | category | flops | bytes accessed | tf_op | source)
XLA Modules:
  0.0 36.1 jit_solution(13061636766742767793)
XLA Ops:
  0.0 35.2 %shard_map.46 = f32[8,10,16,128]{3,2,1,0:T(8,128)S(1)} custom-call(f32[8,10,16,128]{3,2,1,0:T(8,128)} %bitcast.3, f32[2,8,16]{2,1,0:T(8,128)} %wind_hbm.1, f32[2,40,128]{2,1,0:T(8,128)} %constant.4.clone.flow_hbm, f32[2,1,128]{2,1,0:T(1,128)} %constant.5.clone.rate_hbm), custom_call_target="tpu_custom_call" | custom-call | tf_op jit(solution)/shard_map/pallas_call | solution.py:666
  35.2 0.8 %copy.6 = f32[8,16,10,128]{3,1,2,0:T(8,128)} copy(f32[8,16,10,128]{3,1,2,0:T(8,128)S(1)} %bitcast.2) | data formatting | bytes 1310720

commit v6 on v5

--- a/solution.py
+++ b/solution.py
@@ -309,6 +309,17 @@
         for copy, _, has_in in plans[s].get(key, ()):
             under(has_in, copy.wait_recv)
 
+    def drain(s, t):
+        for key, row in plans[s].items():
+            if key[1] == t:
+                for copy, has_out, _ in row:
+                    under(has_out, copy.wait_send)
+        if bending:
+            for c in RELAYED:
+                for out, on, from_here, here in legs(s, t, c):
+                    under(from_here, out.wait_send)
+                    under(here, on.wait_send)
+
     def v_parts(buf, t):
         eps = eps_of(d_speed)
         coef = ACCEL_MAX / (3.0 * d_speed)
@@ -623,21 +634,15 @@
             if s < 2 and t > 0:
                 forward(s + 1, t - 1)
             h_pass(s, t)
+            if s == 2 and t == max(tiles - 2, 0):
+                for copy in rate_copies:
+                    copy.wait_send()
+                for done in range(3 * tiles - 1):
+                    drain(done // tiles, done % tiles)
             if s < 2 and t == 0:
                 v_pass(bufs[s + 1], 0)
 
-    for copy in rate_copies:
-        copy.wait_send()
-    for s in range(3):
-        for row in plans[s].values():
-            for copy, has_out, _ in row:
-                under(has_out, copy.wait_send)
-        if bending:
-            for t in range(tiles):
-                for c in RELAYED:
-                    for out, on, from_here, here in legs(s, t, c):
-                        under(from_here, out.wait_send)
-                        under(here, on.wait_send)
+    drain(2, tiles - 1)
 
 
 def tables(nv, n_head):

time: 36.3 us -> 36.2 us (level)
  no operation moved by 1% of the time
where the time goes in v6:
time: 36.2 us; the launch traced here: 36 us
  Pallas kernels  35.1 us (97%)
  local copies, waits for them, and re-layouts  0.84 us (2%)
    pallas_call x1, Pallas kernels, body(): pl.pallas_call(functools.partial(kernel, (nx, ny, nh, nv), axes), out_sha...  35.1 us
    unnamed x1, local copies, waits for them, and re-layouts  0.84 us

profile of v6, /device:TPU:0, one launch (start us, length us, event | category | flops | bytes accessed | tf_op | source)
XLA Modules:
  0.0 36.0 jit_solution(14717910432713652883)
XLA Ops:
  0.0 35.1 %shard_map.46 = f32[8,10,16,128]{3,2,1,0:T(8,128)S(1)} custom-call(f32[8,10,16,128]{3,2,1,0:T(8,128)} %bitcast.3, f32[2,8,16]{2,1,0:T(8,128)} %wind_hbm.1, f32[2,40,128]{2,1,0:T(8,128)} %constant.4.clone.flow_hbm, f32[2,1,128]{2,1,0:T(1,128)} %constant.5.clone.rate_hbm), custom_call_target="tpu_custom_call" | custom-call | tf_op jit(solution)/shard_map/pallas_call | solution.py:671
  35.1 0.8 %copy.6 = f32[8,16,10,128]{3,1,2,0:T(8,128)} copy(f32[8,16,10,128]{3,1,2,0:T(8,128)S(1)} %bitcast.2) | data formatting | bytes 1310720

commit v7 on v6

--- a/solution.py
+++ b/solution.py
@@ -86,7 +86,7 @@
 
 
 def head_chunks(nh):
-    half = nh // 2
+    half = nh - nh * 2 // 5
     return ((0, half), (half, nh - half))
 
 

time: 36.2 us -> 35.9 us (level)
  no operation moved by 1% of the time
where the time goes in v7:
time: 35.9 us; the launch traced here: 35.7 us
  Pallas kernels  34.9 us (97%)
  local copies, waits for them, and re-layouts  0.84 us (2%)
    pallas_call x1, Pallas kernels, body(): pl.pallas_call(functools.partial(kernel, (nx, ny, nh, nv), axes), out_sha...  34.9 us
    unnamed x1, local copies, waits for them, and re-layouts  0.84 us

profile of v7, /device:TPU:0, one launch (start us, length us, event | category | flops | bytes accessed | tf_op | source)
XLA Modules:
  0.0 35.7 jit_solution(6882881436741922705)
XLA Ops:
  0.0 34.9 %shard_map.46 = f32[8,10,16,128]{3,2,1,0:T(8,128)S(1)} custom-call(f32[8,10,16,128]{3,2,1,0:T(8,128)} %bitcast.3, f32[2,8,16]{2,1,0:T(8,128)} %wind_hbm.1, f32[2,40,128]{2,1,0:T(8,128)} %constant.4.clone.flow_hbm, f32[2,1,128]{2,1,0:T(1,128)} %constant.5.clone.rate_hbm), custom_call_target="tpu_custom_call" | custom-call | tf_op jit(solution)/shard_map/pallas_call | solution.py:671
  34.9 0.8 %copy.6 = f32[8,16,10,128]{3,1,2,0:T(8,128)} copy(f32[8,16,10,128]{3,1,2,0:T(8,128)S(1)} %bitcast.2) | data formatting | bytes 1310720
